TPU v7x, 256 devices: a whole 4x4x8 slice. The times are simulated.
256 devices in a mesh: robot: 64 (over x, z, core), sub: 4 (over y).
Axes of the slice: x: 4, y: 4, z: 8, core: 2. Of those that a mesh axis runs over, the one named last changes fastest.
Arguments:
- landmark_copies: float32 [64, 4, 3, 4096], P('robot', 'sub'), may hold values from -6 to 6
- dual_copies: float32 [64, 4, 3, 4096], P('robot', 'sub'), may hold values from -4 to 4
- visibility: int32 [64, 4, 4096], P('robot', 'sub'), may hold values from 0 to 511
- block_counts: int32 [64, 4, 64], P('robot', 'sub'), may hold values from 1 to 64, as said below
- consensus_old: float32 [64, 4, 3, 512], P('robot', 'sub'), may hold values from -6 to 6
- poses: float32 [64, 4, 6, 1024], P('robot', 'sub'), may hold values from -6 to 6
- inverse_blocks: float32 [64, 4, 36, 1024], P('robot', 'sub'), may hold values from -1.8 to 1.8
- jacobians: float32 [64, 4, 18, 4096], P('robot', 'sub'), may hold values from -3 to 3
- measurements: float32 [64, 4, 3, 4096], P('robot', 'sub'), may hold values from -6 to 6
- obs_pose: int32 [64, 4, 4096], P('robot', 'sub'), may hold values from 0 to 1023
- obs_slot: int32 [64, 4, 4096], P('robot', 'sub'), may hold values from 0 to 4095, as said below
- edge_to: int32 [64, 4, 1024], P('robot', 'sub'), may hold values from 0 to 4095
- edge_offset: float32 [64, 4, 6, 1024], P('robot', 'sub'), may hold values from -3 to 3
Outputs:
- refined_poses: float32 [64, 4, 6, 1024], P('robot', 'sub')
- consensus: float32 [64, 4, 3, 512], P('robot', 'sub')
- dual_new: float32 [64, 4, 3, 4096], P('robot', 'sub')
- residual_norms: float32 [2], replicated
Inputs may be any that keep to these rules, and one draw needn't show every extreme that they name: block_counts[r,s,d] counts the live slots at the head of block d; for every sub index some robot receives full blocks from every robot, which robot varies with the draw. `obs_slot`: each observation names a live slot of its own device.
All inputs are finite; a program needn't handle non-finite values.
Results may differ from a plain program's by a relative error of at most 0.0001.
Values sent between devices are 32-bit elements; how exact they have to be, the bound alone decides.
A program may use at most 64 MiB of HBM per device.

v0:
```python
import jax
import jax.numpy as jnp
from jax import lax
from jax.sharding import Mesh
from jax.sharding import PartitionSpec as P

ROBOT = ("robot_0", "robot_1", "robot_2")
ROBOT_SUB = ("robot_0", "robot_1", "robot_2", "sub")
penalty = 2.0


def over_axes(x, axes):
    for axis in axes:
        x = lax.psum(x, axis)
    return x


def copy_for_each(x, axis):
    length = lax.axis_size(axis)
    return lax.all_to_all(jnp.broadcast_to(x[None], (length, *x.shape)), axis, 0, 0, tiled=True)


def laid_out(pieces, dim):
    dims = list(pieces.shape[1:])
    dims[dim] *= pieces.shape[0]
    return jnp.moveaxis(pieces, 0, dim).reshape(dims)


def collect(x, axis, dim):
    pieces = copy_for_each(x, axis)
    return laid_out(pieces, dim)


def body(
    landmark_copies,
    dual_copies,
    visibility,
    block_counts,
    consensus_old,
    poses,
    inverse_blocks,
    jacobians,
    measurements,
    obs_pose,
    obs_slot,
    edge_to,
    edge_offset,
):
    copies = landmark_copies[0, 0]
    duals = dual_copies[0, 0]
    slot_ids = visibility[0]
    counts = block_counts[0, 0]
    old_estimate = consensus_old[0, 0]
    robots = lax.axis_size(ROBOT)
    slot_count = copies.shape[1]
    block_size = slot_count // robots
    owned = old_estimate.shape[1]
    live_mask = (
        (jnp.arange(block_size)[None, :] < counts[:, None]).reshape(slot_count).astype(jnp.float32)
    )
    outgoing = jnp.concatenate([(copies + duals) * live_mask[None, :], live_mask[None, :]], axis=0)
    received, received_ids = (
        lax.all_to_all(outgoing, ROBOT, split_axis=1, concat_axis=1, tiled=True),
        lax.all_to_all(slot_ids, ROBOT, split_axis=1, concat_axis=1, tiled=True),
    )
    owner_ids = received_ids[0]
    totals = jax.vmap(lambda entries: jax.ops.segment_sum(entries, owner_ids, num_segments=owned))(
        received
    )
    consensus = (old_estimate + totals[:3]) / (1.0 + totals[3:4])
    returning = consensus[:, owner_ids]
    back = lax.all_to_all(returning, ROBOT, split_axis=1, concat_axis=1, tiled=True)
    differ = (copies - back) * live_mask[None, :]
    dual_new = duals + differ
    primal = jnp.sum(differ * differ)
    change = consensus - old_estimate
    dualsum = penalty * penalty * jnp.sum(totals[3:4] * change * change)
    primal_all, dual_all = (over_axes(primal, ROBOT_SUB), over_axes(dualsum, ROBOT_SUB))
    landmark_total = owned * robots * lax.axis_size("sub")
    residual_norms = jnp.sqrt(jnp.stack([primal_all, dual_all]) / landmark_total)
    pose_block = poses[0, 0]
    pose_count = pose_block.shape[1]
    robot_all = collect(pose_block, "sub", 1)
    pose_far = robot_all[:, edge_to[0, 0]]
    copies_at = copies[:, obs_slot[0, 0]]
    error = measurements[0, 0] - copies_at
    jac_rows = jacobians[0, 0].reshape(3, 6, error.shape[1])
    pull = jnp.sum(jac_rows * error[:, None, :], axis=0)
    pose_ids = obs_pose[0, 0]
    grad_obs = jax.vmap(
        lambda entries: jax.ops.segment_sum(entries, pose_ids, num_segments=pose_count)
    )(pull)
    grad = grad_obs + pose_far - pose_block - edge_offset[0, 0]
    inverse = inverse_blocks[0, 0].reshape(6, 6, pose_count)
    delta = jnp.sum(inverse * grad[None, :, :], axis=1)
    refined = pose_block + delta
    return (refined[None, None], consensus[None, None], dual_new[None, None], residual_norms)


def solution(mesh):
    finer = Mesh(
        mesh.devices.reshape(4, 8, 2, mesh.shape["sub"]), ("robot_0", "robot_1", "robot_2", "sub")
    )
    return jax.shard_map(
        body,
        mesh=finer,
        in_specs=(
            P(ROBOT, "sub", None, None),
            P(ROBOT, "sub", None, None),
            P(ROBOT, "sub", None),
            P(ROBOT, "sub", None),
            P(ROBOT, "sub", None, None),
            P(ROBOT, "sub", None, None),
            P(ROBOT, "sub", None, None),
            P(ROBOT, "sub", None, None),
            P(ROBOT, "sub", None, None),
            P(ROBOT, "sub", None),
            P(ROBOT, "sub", None),
            P(ROBOT, "sub", None),
            P(ROBOT, "sub", None, None),
        ),
        out_specs=(
            P(ROBOT, "sub", None, None),
            P(ROBOT, "sub", None, None),
            P(ROBOT, "sub", None, None),
            P(),
        ),
        check_vma=False,
    )
```

profile of v0, /device:TPU:2, one launch (start us, length us, event | category | flops | bytes accessed | tf_op | source)
XLA Modules:
  0.0 214.0 jit_solution(6350417667022919930)
XLA Ops:
  1.2 1.4 reduce.16
  2.6 0.7 all_to_all.26
  3.3 12.0 %all-to-all-start.1 = ((s32[1,64,64]{2,0,1:T(1,128)}), s32[1,64,64]{2,0,1:T(1,128)S(1)}, u32[]{:S(2)}, u32[]{:S(2)}) async-start(s32[1,64,64]{2,0,1:T(1,128)} %all_to_all.26), calls=%async_computation.1 | async-start | bytes 65536 | tf_op jit(solution)/shard_map/all_to_all | solution.py:64
  15.3 0.7 fusion.8
  16.1 0.7 fusion.9
  16.8 1.4 copy.54
  18.6 2.0 copy.53
  20.6 14.1 %gather_fusion.1 = f32[4096,3]{1,0:T(8,128)} fusion(f32[3,4096]{0,1:T(8,128)S(1)} %bitcast.57, s32[4096]{0:T(1024)S(1)} %broadcast_clamp_fusion.1), kind=kCustom, calls=%fused_computation.1 | custom fusion | bytes 114688 | tf_op jit(solution)/shard_map/gather | solution.py:85
  34.6 3.7 %bitcast_subtract_fusion.1 = f32[3,4096]{0,1:T(8,128)} fusion(f32[4096,3]{1,0:T(8,128)} %gather_fusion.1, f32[1,1,3,4096]{2,3,1,0:T(8,128)} %copy.53), kind=kLoop, calls=%fused_computation.9 | loop fusion | flops 12288 | bytes 147456 | tf_op jit(solution)/shard_map/sub | solution.py:86
  38.4 2.3 %copy.55 = f32[3,4096]{1,0:T(4,128)S(1)} copy(f32[3,4096]{0,1:T(8,128)} %bitcast_subtract_fusion.1) | data formatting | bytes 98304 | tf_op jit(solution)/shard_map/sub | solution.py:86
  40.6 0.7 reduce.1
  41.6 0.7 reshape.197
  42.6 0.8 reshape.266
  43.3 0.8 copy.59
  44.2 2.0 copy.56
  46.2 1.0 copy.57
  47.2 1.3 reduce
  48.4 0.7 reshape_squeeze.6
  49.8 4.5 %all-to-all-start = ((f32[4,6,1024]{2,1,0:T(8,128)}), f32[4,6,1024]{2,1,0:T(8,128)S(1)}, u32[]{:S(2)}, u32[]{:S(2)}) async-start(f32[4,6,1024]{2,1,0:T(8,128)} %broadcast_in_dim.9), calls=%async_computation | async-start | bytes 262144 | tf_op jit(solution)/shard_map/all_to_all | solution.py:20
  55.0 0.7 reduce.17
  55.7 0.7 reshape.232
  56.4 3.8 %all-to-all-done = f32[4,6,1024]{2,1,0:T(8,128)S(1)} async-done(((f32[4,6,1024]{2,1,0:T(8,128)}), f32[4,6,1024]{2,1,0:T(8,128)S(1)}, u32[]{:S(2)}, u32[]{:S(2)}) %all-to-all-start) | async-done | bytes 98336 | tf_op jit(solution)/shard_map/all_to_all | solution.py:20
  60.2 10.3 %all-to-all-start.2 = ((f32[64,1,256]{2,1,0:T(1,128)}), f32[64,1,256]{2,1,0:T(1,128)S(1)}, u32[]{:S(2)}, u32[]{:S(2)}) async-start(f32[64,1,256]{2,1,0:T(1,128)} %reshape.266), calls=%async_computation.2 | async-start | bytes 131072 | tf_op jit(solution)/shard_map/all_to_all | solution.py:63
  70.6 1.9 copy.52
  72.5 4.4 %gather_fusion = f32[1024,6]{1,0:T(8,128)S(1)} fusion(f32[6,4096]{0,1:T(8,128)} %bitcast.60, s32[1024]{0:T(1024)S(1)} %broadcast_clamp_fusion.2), kind=kCustom, calls=%fused_computation | custom fusion | bytes 53248 | tf_op jit(solution)/shard_map/gather | solution.py:84
  76.9 22.9 %scatter_fusion = f32[6,1024]{0,1:T(8,128)S(1)} fusion(f32[6,1024]{0,1:T(8,128)S(1)} %bitcast.58, s32[4096]{0:T(1024)} %bitcast.74, f32[4096,6]{1,0:T(8,128)} %copy.56), kind=kCustom, calls=%fused_computation.3 | custom fusion | flops 24576 | bytes 311296 | tf_op jit(solution)/shard_map/vmap()/scatter-add | solution.py:91
  99.8 1.9 bitcast_subtract_fusion.2
  101.7 1.2 copy.58
  102.9 1.0 multiply_reduce_fusion.1
  104.5 0.8 reduce.18
  105.5 2.0 copy.62
  107.5 22.9 %scatter_custom_fusion.1 = f32[4,512]{0,1:T(8,128)S(1)} fusion(s32[4096]{0:T(1024)} %reshape.232, f32[4096,4]{1,0:T(8,128)} %copy.62, f32[]{:T(128)} %constant.9.clone.1), kind=kCustom, calls=%fused_computation.22 | custom fusion | flops 16384 | bytes 8704 | tf_op jit(solution)/shard_map/vmap()/scatter-add | solution.py:67
  130.7 0.8 fusion.3
  131.6 14.1 %gather_fusion.2 = f32[4096,3]{1,0:T(8,128)} fusion(f32[3,512]{0,1:T(8,128)S(1)} %get-tuple-element.31, s32[4096]{0:T(1024)S(1)} %copy-done.6), kind=kCustom, calls=%fused_computation.2 | custom fusion | bytes 114688 | tf_op jit(solution)/shard_map/gather | solution.py:71
  145.6 2.3 %copy.63 = f32[3,64,64]{2,0,1:T(4,128)S(1)} copy(f32[3,64,64]{0,2,1:T(8,128)} %bitcast.61) | data formatting | bytes 98304 | tf_op jit(solution)/shard_map/all_to_all | solution.py:72
  147.9 0.8 reshape.268
  148.7 10.3 %all-to-all-start.3 = ((f32[64,1,192]{2,1,0:T(1,128)}), f32[64,1,192]{2,1,0:T(1,128)S(1)}, u32[]{:S(2)}, u32[]{:S(2)}) async-start(f32[64,1,192]{2,1,0:T(1,128)} %reshape.268), calls=%async_computation.3 | async-start | bytes 131072 | tf_op jit(solution)/shard_map/all_to_all | solution.py:72
  159.6 0.7 copy.68
  161.0 6.8 %all-to-all-done.3 = f32[64,1,192]{2,1,0:T(1,128)S(1)} async-done(((f32[64,1,192]{2,1,0:T(1,128)}), f32[64,1,192]{2,1,0:T(1,128)S(1)}, u32[]{:S(2)}, u32[]{:S(2)}) %all-to-all-start.3) | async-done | bytes 49184 | tf_op jit(solution)/shard_map/all_to_all | solution.py:72
  167.8 0.8 reduce.19
  168.7 2.0 copy.67
  170.9 2.5 %fusion.2 = f32[]{:T(128)} fusion(f32[3,64,64]{0,2,1:T(8,128)} %copy.67, f32[4096]{0:T(1024)S(1)} %copy-done.5, f32[1,1,3,4096]{2,3,1,0:T(8,128)S(1)} %copy.54), kind=kLoop, calls=%fused_computation.8 | loop fusion | flops 49151 | bytes 114692 | tf_op jit(solution)/shard_map/reduce_sum | solution.py:75
  173.5 0.7 copy.69
  174.2 9.8 %all-reduce.2 = (f32[]{:T(128)}, f32[]{:T(128)}) all-reduce(f32[]{:T(128)S(6)} %mul_shard_map.3, f32[]{:T(128)} %fusion.2), channel_id=1, replica_groups=mesh['robot_0'=4,'robot_1'=8,'robot_2'=2,'sub'=4] {'robot_0'}, use_global_device_ids=true, to_apply=%region_10.0 | all-reduce | flops 2 | bytes 16 | tf_op jit(solution)/shard_map/psum | solution.py:14
  184.0 15.5 %all-reduce = (f32[]{:T(128)}, f32[]{:T(128)}) all-reduce(f32[]{:T(128)} %get-tuple-element.26, f32[]{:T(128)} %get-tuple-element.27), channel_id=1, replica_groups=mesh['robot_0'=4,'robot_1'=8,'robot_2'=2,'sub'=4] {'robot_1'}, use_global_device_ids=true, to_apply=%region_11.0 | all-reduce | flops 2 | bytes 16 | tf_op jit(solution)/shard_map/psum | solution.py:14
  199.5 3.2 %all-reduce.3 = (f32[]{:T(128)}, f32[]{:T(128)}) all-reduce(f32[]{:T(128)} %get-tuple-element.22, f32[]{:T(128)} %get-tuple-element.23), channel_id=1, replica_groups=mesh['robot_0'=4,'robot_1'=8,'robot_2'=2,'sub'=4] {'robot_2'}, use_global_device_ids=true, to_apply=%region_12.0 | all-reduce | flops 2 | bytes 16 | tf_op jit(solution)/shard_map/psum | solution.py:14
  202.7 9.5 %all-reduce.1 = (f32[1]{0:T(128)}, f32[1]{0:T(128)}) all-reduce(f32[1]{0:T(128)} %bitcast.24, f32[1]{0:T(128)} %bitcast.23), channel_id=1, replica_groups=mesh['robot_0'=4,'robot_1'=8,'robot_2'=2,'sub'=4] {'sub'}, use_global_device_ids=true, to_apply=%region_13.0 | all-reduce | flops 2 | bytes 16 | tf_op jit(solution)/shard_map/psum | solution.py:14
  212.2 1.8 fusion.10
  (52 shorter events, 4.7 us)
Async XLA Ops:
  0.6 17.6 %copy-start = (f32[1,1,3,4096]{3,1,2,0:T(1,128)S(1)}, f32[1,1,3,4096]{3,1,2,0:T(1,128)}, u32[]{:S(2)}) copy-start(f32[1,1,3,4096]{3,1,2,0:T(1,128)} %param.13) | copy-start | bytes 147460
  0.6 17.6 %copy-start.3 = (f32[1,1,3,4096]{3,1,2,0:T(1,128)S(1)}, f32[1,1,3,4096]{3,1,2,0:T(1,128)}, u32[]{:S(2)}) copy-start(f32[1,1,3,4096]{3,1,2,0:T(1,128)} %param.14) | copy-start | bytes 147460
  0.7 17.9 %copy-start.9 = (s32[1,1,4096]{2,1,0:T(1,128)S(1)}, s32[1,1,4096]{2,1,0:T(1,128)}, u32[]{:S(2)}) copy-start(s32[1,1,4096]{2,1,0:T(1,128)} %param.23) | copy-start | bytes 49156
  0.7 17.9 %copy-start.7 = (f32[1,1,3,4096]{3,1,2,0:T(1,128)S(1)}, f32[1,1,3,4096]{3,1,2,0:T(1,128)}, u32[]{:S(2)}) copy-start(f32[1,1,3,4096]{3,1,2,0:T(1,128)} %param.21) | copy-start | bytes 147460
  3.3 45.8 %all-to-all-start.1 = ((s32[1,64,64]{2,0,1:T(1,128)}), s32[1,64,64]{2,0,1:T(1,128)S(1)}, u32[]{:S(2)}, u32[]{:S(2)}) async-start(s32[1,64,64]{2,0,1:T(1,128)} %all_to_all.26), calls=%async_computation.1 | async-start | bytes 65536 | tf_op jit(solution)/shard_map/all_to_all | solution.py:64
  38.4 2.3 %copy-start.1 = (f32[1,1,18,4096]{3,1,2,0:T(1,128)S(1)}, f32[1,1,18,4096]{3,1,2,0:T(1,128)}, u32[]{:S(2)}) copy-start(f32[1,1,18,4096]{3,1,2,0:T(1,128)} %param.20) | copy-start | bytes 884740
  38.4 3.0 %copy-start.10 = (s32[1,1,1024]{2,1,0:T(1,128)S(1)}, s32[1,1,1024]{2,1,0:T(1,128)}, u32[]{:S(2)}) copy-start(s32[1,1,1024]{2,1,0:T(1,128)} %param.24) | copy-start | bytes 12292
  38.4 3.9 %copy-start.2 = (f32[1,1,6,1024]{3,1,2,0:T(1,128)S(1)}, f32[1,1,6,1024]{3,1,2,0:T(1,128)}, u32[]{:S(2)}) copy-start(f32[1,1,6,1024]{3,1,2,0:T(1,128)} %param.18) | copy-start | bytes 73732
  41.5 4.6 %copy-start.8 = (f32[1,1,6,1024]{3,1,2,0:T(1,128)S(1)}, f32[1,1,6,1024]{3,1,2,0:T(1,128)}, u32[]{:S(2)}) copy-start(f32[1,1,6,1024]{3,1,2,0:T(1,128)} %param.25) | copy-start | bytes 73732
  49.8 10.4 %all-to-all-start = ((f32[4,6,1024]{2,1,0:T(8,128)}), f32[4,6,1024]{2,1,0:T(8,128)S(1)}, u32[]{:S(2)}, u32[]{:S(2)}) async-start(f32[4,6,1024]{2,1,0:T(8,128)} %broadcast_in_dim.9), calls=%async_computation | async-start | bytes 262144 | tf_op jit(solution)/shard_map/all_to_all | solution.py:20
  60.2 43.7 %all-to-all-start.2 = ((f32[64,1,256]{2,1,0:T(1,128)}), f32[64,1,256]{2,1,0:T(1,128)S(1)}, u32[]{:S(2)}, u32[]{:S(2)}) async-start(f32[64,1,256]{2,1,0:T(1,128)} %reshape.266), calls=%async_computation.2 | async-start | bytes 131072 | tf_op jit(solution)/shard_map/all_to_all | solution.py:63
  105.3 26.3 %copy-start.6 = (s32[4096]{0:T(1024)S(1)}, s32[4096]{0:T(1024)}, u32[]{:S(2)}) copy-start(s32[4096]{0:T(1024)} %broadcast_clamp_fusion) | copy-start | bytes 49156
  147.9 23.0 %copy-start.5 = (f32[4096]{0:T(1024)S(1)}, f32[4096]{0:T(1024)}, u32[]{:S(2)}) copy-start(f32[4096]{0:T(1024)} %reshape.197) | copy-start | bytes 49156
  148.7 19.1 %all-to-all-start.3 = ((f32[64,1,192]{2,1,0:T(1,128)}), f32[64,1,192]{2,1,0:T(1,128)S(1)}, u32[]{:S(2)}, u32[]{:S(2)}) async-start(f32[64,1,192]{2,1,0:T(1,128)} %reshape.268), calls=%async_computation.3 | async-start | bytes 131072 | tf_op jit(solution)/shard_map/all_to_all | solution.py:72
  170.9 2.6 %copy-start.4 = (f32[1,1,3,4096]{3,1,2,0:T(1,128)S(1)}, f32[1,1,3,4096]{3,1,2,0:T(1,128)}, u32[]{:S(2)}) copy-start(f32[1,1,3,4096]{3,1,2,0:T(1,128)} %param.14) | copy-start | bytes 147460
where the time goes:
time: 215 us; the launch traced here: 214 us
  other arithmetic  66.6 us (31%)
  local copies, waits for them, and re-layouts  59.9 us (28%)
  blocking collectives  38 us (18%)
  starting transfers between devices  37.1 us (17%)
  waiting for transfers between devices  10.7 us (5%)
    psum x4, blocking collectives, over_axes(): x = lax.psum(x, axis)  38 us
    scatter-add x1, other arithmetic, body(): jax.ops.segment_sum(entries, owner_ids, num_segments=owned)  22.9 us
    scatter-add x1, other arithmetic, body(): jax.ops.segment_sum(entries, pose_ids, num_segments=pose_count)  22.9 us
    gather x1, local copies, waits for them, and re-layouts, body(): copies_at = copies[:, obs_slot[0, 0]]  14.1 us
    gather x1, local copies, waits for them, and re-layouts, body(): returning = consensus[:, owner_ids]  14.1 us
    all_to_all x1, starting transfers between devices, body(): lax.all_to_all(slot_ids, ROBOT, split_axis=1, concat_axis=1, tiled=True)  12 us
    all_to_all x1, starting transfers between devices, body(): lax.all_to_all(returning, ROBOT, split_axis=1, concat_axis=1, tiled=True)  10.3 us
    all_to_all x1, starting transfers between devices, body(): lax.all_to_all(outgoing, ROBOT, split_axis=1, concat_axis=1, tiled=True)  10.3 us
  transfers between devices with their start and end apart: 4, of which 2 were waited for; matrix products, arithmetic and copies ran while one was open for 33% of the time, Pallas kernels for 0%

commit v1 on v0

--- a/solution.py
+++ b/solution.py
@@ -11,7 +11,8 @@
 
 def over_axes(x, axes):
     for axis in axes:
-        x = lax.psum(x, axis)
+        parts = lax.all_gather(x, axis, axis=0, tiled=False)
+        x = parts.sum(axis=0)
     return x
 
 

time: 215 us -> 231 us (1.074)
  local copies, waits for them, and re-layouts: 59.9 us -> 74.7 us
  other arithmetic: 66.6 us -> 71.6 us
  blocking collectives: 38 us -> 35.3 us
    psum x4 -> x0, blocking collectives: 38 us -> none  [over_axes(): x = lax.psum(x, axis)]
    unnamed x0 -> x4, blocking collectives: none -> 35.3 us
    unnamed x34 -> x56, local copies, waits for them, and re-layouts: 9.16 us -> 23.9 us
    reduce_sum x0 -> x8, other arithmetic: none -> 4.88 us  [over_axes(): x = parts.sum(axis=0)]
where the time goes in v1:
time: 231 us; the launch traced here: 230 us
  local copies, waits for them, and re-layouts  74.7 us (32%)
  other arithmetic  71.6 us (31%)
  starting transfers between devices  37.1 us (16%)
  blocking collectives  35.3 us (15%)
  waiting for transfers between devices  9.95 us (4%)
    unnamed x4, blocking collectives  35.3 us
    unnamed x56, local copies, waits for them, and re-layouts  23.9 us
    scatter-add x1, other arithmetic, body(): jax.ops.segment_sum(entries, owner_ids, num_segments=owned)  22.9 us
    scatter-add x1, other arithmetic, body(): jax.ops.segment_sum(entries, pose_ids, num_segments=pose_count)  22.9 us
    gather x1, local copies, waits for them, and re-layouts, body(): copies_at = copies[:, obs_slot[0, 0]]  14.1 us
    gather x1, local copies, waits for them, and re-layouts, body(): returning = consensus[:, owner_ids]  14.1 us
    all_to_all x1, starting transfers between devices, body(): lax.all_to_all(slot_ids, ROBOT, split_axis=1, concat_axis=1, tiled=True)  12 us
    all_to_all x1, starting transfers between devices, body(): lax.all_to_all(returning, ROBOT, split_axis=1, concat_axis=1, tiled=True)  10.3 us
  transfers between devices with their start and end apart: 4, of which 2 were waited for; matrix products, arithmetic and copies ran while one was open for 33% of the time, Pallas kernels for 0%

profile of v1, /device:TPU:2, one launch (start us, length us, event | category | flops | bytes accessed | tf_op | source)
XLA Modules:
  0.0 230.3 jit_solution(12217671549824149363)
XLA Ops:
  1.2 1.4 reduce.24
  3.3 12.0 %all-to-all-start.1 = ((s32[1,64,64]{2,0,1:T(1,128)}), s32[1,64,64]{2,0,1:T(1,128)S(1)}, u32[]{:S(2)}, u32[]{:S(2)}) async-start(s32[1,64,64]{2,0,1:T(1,128)} %all_to_all.26), calls=%async_computation.1 | async-start | bytes 65536 | tf_op jit(solution)/shard_map/all_to_all | solution.py:65
  16.8 1.4 copy.54
  18.6 2.0 copy.53
  20.6 14.1 %gather_fusion.1 = f32[4096,3]{1,0:T(8,128)} fusion(f32[3,4096]{0,1:T(8,128)S(1)} %bitcast.69, s32[4096]{0:T(1024)S(1)} %broadcast_clamp_fusion.1), kind=kCustom, calls=%fused_computation.1 | custom fusion | bytes 114688 | tf_op jit(solution)/shard_map/gather | solution.py:86
  34.6 3.7 %bitcast_subtract_fusion.1 = f32[3,4096]{0,1:T(8,128)} fusion(f32[4096,3]{1,0:T(8,128)} %gather_fusion.1, f32[1,1,3,4096]{2,3,1,0:T(8,128)} %copy.53), kind=kLoop, calls=%fused_computation.9 | loop fusion | flops 12288 | bytes 147456 | tf_op jit(solution)/shard_map/sub | solution.py:87
  38.4 2.3 copy.55
  42.6 0.8 reshape.306
  43.3 0.8 copy.59
  44.2 1.3 dynamic-slice
  45.5 1.3 dynamic-slice.1
  46.7 1.2 dynamic-slice.2
  48.7 2.0 copy.56
  50.7 1.0 copy.57
  51.7 1.3 reduce.8
  54.3 4.5 %all-to-all-start = ((f32[4,6,1024]{2,1,0:T(8,128)}), f32[4,6,1024]{2,1,0:T(8,128)S(1)}, u32[]{:S(2)}, u32[]{:S(2)}) async-start(f32[4,6,1024]{2,1,0:T(8,128)} %broadcast_in_dim.9), calls=%async_computation | async-start | bytes 262144 | tf_op jit(solution)/shard_map/all_to_all | solution.py:21
  60.9 3.8 %all-to-all-done = f32[4,6,1024]{2,1,0:T(8,128)S(1)} async-done(((f32[4,6,1024]{2,1,0:T(8,128)}), f32[4,6,1024]{2,1,0:T(8,128)S(1)}, u32[]{:S(2)}, u32[]{:S(2)}) %all-to-all-start) | async-done | bytes 98336 | tf_op jit(solution)/shard_map/all_to_all | solution.py:21
  64.7 10.3 %all-to-all-start.2 = ((f32[64,1,256]{2,1,0:T(1,128)}), f32[64,1,256]{2,1,0:T(1,128)S(1)}, u32[]{:S(2)}, u32[]{:S(2)}) async-start(f32[64,1,256]{2,1,0:T(1,128)} %reshape.306), calls=%async_computation.2 | async-start | bytes 131072 | tf_op jit(solution)/shard_map/all_to_all | solution.py:64
  75.1 1.9 copy.52
  77.0 4.4 %gather_fusion = f32[1024,6]{1,0:T(8,128)S(1)} fusion(f32[6,4096]{0,1:T(8,128)} %bitcast.72, s32[1024]{0:T(1024)S(1)} %broadcast_clamp_fusion.2), kind=kCustom, calls=%fused_computation | custom fusion | bytes 53248 | tf_op jit(solution)/shard_map/gather | solution.py:85
  81.4 22.9 %scatter_fusion = f32[6,1024]{0,1:T(8,128)S(1)} fusion(f32[6,1024]{0,1:T(8,128)S(1)} %bitcast.70, s32[4096]{0:T(1024)} %bitcast.86, f32[4096,6]{1,0:T(8,128)} %copy.56), kind=kCustom, calls=%fused_computation.3 | custom fusion | flops 24576 | bytes 311296 | tf_op jit(solution)/shard_map/vmap()/scatter-add | solution.py:92
  104.3 1.9 bitcast_subtract_fusion.2
  106.2 1.2 copy.58
  107.4 1.0 multiply_reduce_fusion.1
  109.0 0.8 reduce.26
  110.0 2.0 copy.62
  112.0 22.9 %scatter_custom_fusion.1 = f32[4,512]{0,1:T(8,128)S(1)} fusion(s32[4096]{0:T(1024)} %reshape.232, f32[4096,4]{1,0:T(8,128)} %copy.62, f32[]{:T(128)} %constant.9.clone.1), kind=kCustom, calls=%fused_computation.22 | custom fusion | flops 16384 | bytes 8704 | tf_op jit(solution)/shard_map/vmap()/scatter-add | solution.py:68
  135.2 0.8 fusion.3
  136.1 14.1 %gather_fusion.2 = f32[4096,3]{1,0:T(8,128)} fusion(f32[3,512]{0,1:T(8,128)S(1)} %get-tuple-element.31, s32[4096]{0:T(1024)S(1)} %copy-done.6), kind=kCustom, calls=%fused_computation.2 | custom fusion | bytes 114688 | tf_op jit(solution)/shard_map/gather | solution.py:72
  150.1 2.3 copy.63
  152.4 0.8 reshape.308
  153.2 10.3 %all-to-all-start.3 = ((f32[64,1,192]{2,1,0:T(1,128)}), f32[64,1,192]{2,1,0:T(1,128)S(1)}, u32[]{:S(2)}, u32[]{:S(2)}) async-start(f32[64,1,192]{2,1,0:T(1,128)} %reshape.308), calls=%async_computation.3 | async-start | bytes 131072 | tf_op jit(solution)/shard_map/all_to_all | solution.py:73
  166.2 6.1 %all-to-all-done.3 = f32[64,1,192]{2,1,0:T(1,128)S(1)} async-done(((f32[64,1,192]{2,1,0:T(1,128)}), f32[64,1,192]{2,1,0:T(1,128)S(1)}, u32[]{:S(2)}, u32[]{:S(2)}) %all-to-all-start.3) | async-done | bytes 49184 | tf_op jit(solution)/shard_map/all_to_all | solution.py:73
  172.3 0.8 reduce.27
  173.2 2.0 copy.67
  175.3 2.5 %fusion.2 = f32[]{:T(128)} fusion(f32[3,64,64]{0,2,1:T(8,128)} %copy.67, f32[4096]{0:T(1024)S(1)} %copy-done.5, f32[1,1,3,4096]{2,3,1,0:T(8,128)S(1)} %copy.54), kind=kLoop, calls=%fused_computation.8 | loop fusion | flops 49151 | bytes 114692 | tf_op jit(solution)/shard_map/reduce_sum | solution.py:76
  177.8 1.4 dynamic-update-slice
  179.2 9.1 %all-reduce.10 = (f32[4]{0:T(128)S(1)}, f32[4]{0:T(128)S(1)}) all-reduce(f32[4]{0:T(128)S(1)} %dynamic-update-slice.4, f32[4]{0:T(128)S(1)} %dynamic-update-slice), channel_id=1, replica_groups=mesh['robot_0'=4,'robot_1'=8,'robot_2'=2,'sub'=4] {'robot_0'}, use_global_device_ids=true, to_apply=%add.4 | all-reduce | flops 8 | bytes 64
  189.5 1.3 dynamic-update-slice.1
  190.8 1.3 dynamic-update-slice.5
  192.2 14.9 %all-reduce.8 = (f32[8]{0:T(128)S(1)}, f32[8]{0:T(128)S(1)}) all-reduce(f32[8]{0:T(128)S(1)} %dynamic-update-slice.5, f32[8]{0:T(128)S(1)} %dynamic-update-slice.1), channel_id=1, replica_groups=mesh['robot_0'=4,'robot_1'=8,'robot_2'=2,'sub'=4] {'robot_1'}, use_global_device_ids=true, to_apply=%add.5 | all-reduce | flops 16 | bytes 128
  208.3 1.3 dynamic-update-slice.2
  209.6 1.3 dynamic-update-slice.6
  211.0 2.5 %all-reduce.11 = (f32[2]{0:T(128)S(1)}, f32[2]{0:T(128)S(1)}) all-reduce(f32[2]{0:T(128)S(1)} %dynamic-update-slice.6, f32[2]{0:T(128)S(1)} %dynamic-update-slice.2), channel_id=1, replica_groups=mesh['robot_0'=4,'robot_1'=8,'robot_2'=2,'sub'=4] {'robot_2'}, use_global_device_ids=true, to_apply=%add.6 | all-reduce | flops 4 | bytes 32
  214.7 1.4 dynamic-update-slice.3
  216.2 1.4 dynamic-update-slice.7
  218.3 8.9 %all-reduce.9 = (f32[4]{0:T(128)S(1)}, f32[4]{0:T(128)S(1)}) all-reduce(f32[4]{0:T(128)S(1)} %dynamic-update-slice.7, f32[4]{0:T(128)S(1)} %dynamic-update-slice.3), channel_id=1, replica_groups=mesh['robot_0'=4,'robot_1'=8,'robot_2'=2,'sub'=4] {'sub'}, use_global_device_ids=true, to_apply=%add.7 | all-reduce | flops 8 | bytes 64
  228.4 1.8 fusion.10
  (82 shorter events, 18.0 us)
Async XLA Ops:
  0.6 17.6 %copy-start = (f32[1,1,3,4096]{3,1,2,0:T(1,128)S(1)}, f32[1,1,3,4096]{3,1,2,0:T(1,128)}, u32[]{:S(2)}) copy-start(f32[1,1,3,4096]{3,1,2,0:T(1,128)} %param.13) | copy-start | bytes 147460
  0.6 17.6 %copy-start.3 = (f32[1,1,3,4096]{3,1,2,0:T(1,128)S(1)}, f32[1,1,3,4096]{3,1,2,0:T(1,128)}, u32[]{:S(2)}) copy-start(f32[1,1,3,4096]{3,1,2,0:T(1,128)} %param.14) | copy-start | bytes 147460
  0.7 17.9 %copy-start.9 = (s32[1,1,4096]{2,1,0:T(1,128)S(1)}, s32[1,1,4096]{2,1,0:T(1,128)}, u32[]{:S(2)}) copy-start(s32[1,1,4096]{2,1,0:T(1,128)} %param.23) | copy-start | bytes 49156
  0.7 17.9 %copy-start.7 = (f32[1,1,3,4096]{3,1,2,0:T(1,128)S(1)}, f32[1,1,3,4096]{3,1,2,0:T(1,128)}, u32[]{:S(2)}) copy-start(f32[1,1,3,4096]{3,1,2,0:T(1,128)} %param.21) | copy-start | bytes 147460
  3.3 50.3 %all-to-all-start.1 = ((s32[1,64,64]{2,0,1:T(1,128)}), s32[1,64,64]{2,0,1:T(1,128)S(1)}, u32[]{:S(2)}, u32[]{:S(2)}) async-start(s32[1,64,64]{2,0,1:T(1,128)} %all_to_all.26), calls=%async_computation.1 | async-start | bytes 65536 | tf_op jit(solution)/shard_map/all_to_all | solution.py:65
  38.4 2.3 copy-start.1
  38.4 3.0 %copy-start.10 = (s32[1,1,1024]{2,1,0:T(1,128)S(1)}, s32[1,1,1024]{2,1,0:T(1,128)}, u32[]{:S(2)}) copy-start(s32[1,1,1024]{2,1,0:T(1,128)} %param.24) | copy-start | bytes 12292
  38.4 3.9 %copy-start.2 = (f32[1,1,6,1024]{3,1,2,0:T(1,128)S(1)}, f32[1,1,6,1024]{3,1,2,0:T(1,128)}, u32[]{:S(2)}) copy-start(f32[1,1,6,1024]{3,1,2,0:T(1,128)} %param.18) | copy-start | bytes 73732
  40.6 7.4 %copy-start.11 = (u32[256]{0:T(256)S(1)}, u32[256]{0:T(256)}, u32[]{:S(2)}) copy-start(u32[256]{0:T(256)} %constant.49) | copy-start | bytes 3076
  41.5 9.1 %copy-start.8 = (f32[1,1,6,1024]{3,1,2,0:T(1,128)S(1)}, f32[1,1,6,1024]{3,1,2,0:T(1,128)}, u32[]{:S(2)}) copy-start(f32[1,1,6,1024]{3,1,2,0:T(1,128)} %param.25) | copy-start | bytes 73732
  54.3 10.4 %all-to-all-start = ((f32[4,6,1024]{2,1,0:T(8,128)}), f32[4,6,1024]{2,1,0:T(8,128)S(1)}, u32[]{:S(2)}, u32[]{:S(2)}) async-start(f32[4,6,1024]{2,1,0:T(8,128)} %broadcast_in_dim.9), calls=%async_computation | async-start | bytes 262144 | tf_op jit(solution)/shard_map/all_to_all | solution.py:21
  64.7 43.7 %all-to-all-start.2 = ((f32[64,1,256]{2,1,0:T(1,128)}), f32[64,1,256]{2,1,0:T(1,128)S(1)}, u32[]{:S(2)}, u32[]{:S(2)}) async-start(f32[64,1,256]{2,1,0:T(1,128)} %reshape.306), calls=%async_computation.2 | async-start | bytes 131072 | tf_op jit(solution)/shard_map/all_to_all | solution.py:64
  109.8 26.3 %copy-start.6 = (s32[4096]{0:T(1024)S(1)}, s32[4096]{0:T(1024)}, u32[]{:S(2)}) copy-start(s32[4096]{0:T(1024)} %broadcast_clamp_fusion) | copy-start | bytes 49156
  152.4 22.9 %copy-start.5 = (f32[4096]{0:T(1024)S(1)}, f32[4096]{0:T(1024)}, u32[]{:S(2)}) copy-start(f32[4096]{0:T(1024)} %reshape.197) | copy-start | bytes 49156
  153.2 19.1 %all-to-all-start.3 = ((f32[64,1,192]{2,1,0:T(1,128)}), f32[64,1,192]{2,1,0:T(1,128)S(1)}, u32[]{:S(2)}, u32[]{:S(2)}) async-start(f32[64,1,192]{2,1,0:T(1,128)} %reshape.308), calls=%async_computation.3 | async-start | bytes 131072 | tf_op jit(solution)/shard_map/all_to_all | solution.py:73
  175.3 35.7 %copy-start.4 = (f32[1,1,3,4096]{3,1,2,0:T(1,128)S(1)}, f32[1,1,3,4096]{3,1,2,0:T(1,128)}, u32[]{:S(2)}) copy-start(f32[1,1,3,4096]{3,1,2,0:T(1,128)} %param.14) | copy-start | bytes 147460
